TPU v7x, 32 devices: a whole 2x2x4 slice. The times are simulated.
32 devices in a mesh: fsdp: 4 (over z), ctx: 2 (over x), tp: 4 (over y, core).
Axes of the slice: x: 2, y: 2, z: 4, core: 2. Of those that a mesh axis runs over, the one named last changes fastest.
Arguments:
- residual: bfloat16 [8, 1024, 1024], P('fsdp', ('ctx', 'tp')), may hold values from -6 to 6
- query_weight: bfloat16 [1024, 1024], P('fsdp', 'tp'), may hold values from -0.1875 to 0.1875
- key_weight: bfloat16 [1024, 1024], P('fsdp', 'tp'), may hold values from -0.1875 to 0.1875
- value_weight: bfloat16 [1024, 1024], P('fsdp', 'tp'), may hold values from -0.1875 to 0.1875
- output_weight: bfloat16 [1024, 1024], P('tp', 'fsdp'), may hold values from -0.1875 to 0.1875
- sharpness: float32 [1024], P('tp'), may hold values from 1 to 1.8
- attend_rate: float32 [1024], replicated, may hold values from 0.15 to 0.9
- up_weight: bfloat16 [1024, 4096], P('fsdp', 'tp'), may hold values from -0.1875 to 0.1875
- gate_weight: bfloat16 [1024, 4096], P('fsdp', 'tp'), may hold values from -0.1875 to 0.1875
- down_weight: bfloat16 [4096, 1024], P('tp', 'fsdp'), may hold values from -0.09375 to 0.09375
- amplitude: float32 [4096], P('tp'), may hold values from 0.5 to 2
- steepness: float32 [4096], P('tp'), may hold values from 0.5 to 2
- mixer_rate: float32 [1024], replicated, may hold values from 0.15 to 0.9
- block_ids: int32 [8, 1024], P('fsdp'), may hold values from 0 to 4, as said below
- positions: int32 [8, 1024], P('fsdp', 'ctx'), may hold values from 0 to 4095
- cotangent: bfloat16 [8, 1024, 1024], P('fsdp', ('ctx', 'tp')), may hold values from -6 to 6
Outputs:
- layer_out: bfloat16 [8, 1024, 1024], P('fsdp', ('ctx', 'tp'))
- grad_input: float32 [8, 1024, 1024], P('fsdp', ('ctx', 'tp'))
- grad_query: float32 [1024, 1024], P('fsdp', 'tp')
- grad_key: float32 [1024, 1024], P('fsdp', 'tp')
- grad_value: float32 [1024, 1024], P('fsdp', 'tp')
- grad_output: float32 [1024, 1024], P('tp', 'fsdp')
- grad_sharpness: float32 [1024], replicated
- grad_attend: float32 [1024], replicated
- grad_up: float32 [1024, 4096], P('fsdp', 'tp')
- grad_gate: float32 [1024, 4096], P('fsdp', 'tp')
- grad_down: float32 [4096, 1024], P('tp', 'fsdp')
- grad_amplitude: float32 [4096], replicated
- grad_steepness: float32 [4096], replicated
- grad_mixer: float32 [1024], replicated
Inputs may be any that keep to these rules, and one draw needn't show every extreme that they name: `block_ids`: in each sequence the block id of the token at index t is (t + offset) // 256, with an offset of 1 to 255 drawn for each sequence: full blocks of 256 tokens, a shorter first and last block.
All inputs are finite; a program needn't handle non-finite values.
Results may differ from a plain program's by a relative error of at most 0.02.
Values may be sent and summed in bfloat16 or wider, within the bound.
A program may use at most 128 MiB of HBM per device.

v0:
```python
import math
import jax
import jax.numpy as jnp
from jax import lax
from jax.sharding import PartitionSpec as P

HD = 64
norm_eps = 1e-06
rope_base = 10000.0
BF = jnp.bfloat16
F32 = jnp.float32


def unit_rows(values):
    return values * lax.rsqrt(jnp.mean(values * values, axis=-1, keepdims=True) + norm_eps)


def rotate_pairs(values, angles):
    middle = values.shape[-1] // 2
    leading = values[..., :middle]
    trailing = values[..., middle:]
    cosine = jnp.cos(angles)[..., None, :]
    sine_part = jnp.sin(angles)[..., None, :]
    return jnp.concatenate(
        [leading * cosine - trailing * sine_part, trailing * cosine + leading * sine_part], axis=-1
    )


def angles_for(positions, head_size):
    middle = head_size // 2
    frequency = rope_base ** (-2.0 * jnp.arange(middle).astype(F32) / head_size)
    return positions.astype(F32)[..., None] * frequency


def prepare_heads(projected, angles, gains, head_size):
    heads_here = projected.shape[-1] // head_size
    shaped = projected.reshape(projected.shape[:-1] + (heads_here, head_size))
    normed = unit_rows(rotate_pairs(shaped, angles)) * gains.reshape(heads_here, head_size)
    return normed.reshape(projected.shape)


def product(left, right):
    return jnp.dot(left, right, preferred_element_type=F32)


def transposed_left(left, right):
    return lax.dot_general(left, right, (((0,), (0,)), ((), ())), preferred_element_type=F32)


def transposed_right(left, right):
    return lax.dot_general(left, right, (((1,), (1,)), ((), ())), preferred_element_type=F32)


def gather_rows(values):
    return lax.all_gather(values, "tp", axis=1, tiled=True)


def reduce_rows(values):
    return lax.psum_scatter(values.astype(BF), "tp", scatter_dimension=1, tiled=True).astype(F32)


def branch_mix(branch, base, rate):
    return unit_rows(base + rate * (unit_rows(branch) - base))


def activate(upper, gated_raw, amplitude, steepness):
    scaled = gated_raw * steepness
    return upper * amplitude * (scaled * jax.nn.sigmoid(scaled))


def trade(values, sizes):
    n = sizes["ctx"]
    me = lax.axis_index("ctx")
    if n == 2:
        own = lax.dynamic_index_in_dim(values, me, 0, keepdims=False)
        other = lax.dynamic_index_in_dim(values, 1 - me, 0, keepdims=False)
        got = lax.ppermute(other, "ctx", [(0, 1), (1, 0)])
        first = jnp.where(me == 0, own, got)
        second = jnp.where(me == 0, got, own)
        return jnp.stack([first, second])
    return lax.all_to_all(values, "ctx", split_axis=0, concat_axis=0, tiled=True)


def attend_both(query_low, key_low, value_low, ids):
    length, width = query_low.shape
    heads = width // HD
    q = query_low.reshape(length, heads, HD)
    k = key_low.reshape(length, heads, HD)
    v = value_low.reshape(length, heads, HD)
    scores = jnp.einsum("qhd,khd->hqk", q, k, preferred_element_type=F32) / math.sqrt(HD)
    allowed = ids[None, :] <= ids[:, None]
    scores = jnp.where(allowed[None], scores, -1e30)
    row_max = jnp.max(scores, axis=-1, keepdims=True)
    exponent = jnp.exp(scores - row_max)
    row_total = jnp.sum(exponent, axis=-1, keepdims=True)
    weights_low = (exponent / row_total).astype(BF)
    out = jnp.einsum("hqk,khd->qhd", weights_low, v, preferred_element_type=F32)
    return (out.reshape(length, width).astype(BF), (row_max + jnp.log(row_total))[..., 0])


def attend_back(query_low, key_low, value_low, ids, logsum, grad):
    length, width = query_low.shape
    heads = width // HD
    q = query_low.reshape(length, heads, HD)
    k = key_low.reshape(length, heads, HD)
    v = value_low.reshape(length, heads, HD)
    g = grad.reshape(length, heads, HD)
    scores = jnp.einsum("qhd,khd->hqk", q, k, preferred_element_type=F32) / math.sqrt(HD)
    allowed = ids[None, :] <= ids[:, None]
    scores = jnp.where(allowed[None], scores, -1e30)
    soft = jnp.exp(scores - logsum[..., None])
    grad_v = jnp.einsum("hqk,qhd->khd", soft.astype(BF), g, preferred_element_type=F32)
    grad_w = jnp.einsum("qhd,khd->hqk", g, v, preferred_element_type=F32)
    grad_s = soft * (grad_w - jnp.sum(grad_w * soft, axis=-1, keepdims=True))
    low = grad_s.astype(BF)
    grad_q = jnp.einsum("hqk,khd->qhd", low, k, preferred_element_type=F32) / math.sqrt(HD)
    grad_k = jnp.einsum("hqk,qhd->khd", low, q, preferred_element_type=F32) / math.sqrt(HD)
    return (
        grad_q.reshape(length, width),
        grad_k.reshape(length, width),
        grad_v.reshape(length, width),
    )


def per_device(sizes):

    def run(
        residual,
        query_weight,
        key_weight,
        value_weight,
        output_weight,
        sharpness,
        attend_rate,
        up_weight,
        gate_weight,
        down_weight,
        amplitude,
        steepness,
        mixer_rate,
        block_ids,
        positions,
        cotangent,
    ):
        z = sizes["fsdp"]
        width = residual.shape[2]
        hidden_here = up_weight.shape[1]
        heads_width = query_weight.shape[1]
        mine = trade(residual, sizes)
        qkv_shard = jnp.concatenate([query_weight, key_weight, value_weight], axis=1)
        full_qkv = lax.all_gather(qkv_shard, "fsdp", axis=0, tiled=True)
        full_output = lax.all_gather(output_weight, "fsdp", axis=1, tiled=True)
        ug_shard = jnp.concatenate([up_weight, gate_weight], axis=1)
        full_ug = lax.all_gather(ug_shard, "fsdp", axis=0, tiled=True)
        full_down = lax.all_gather(down_weight, "fsdp", axis=1, tiled=True)
        ctx = lax.axis_index("ctx")
        ids = lax.dynamic_index_in_dim(block_ids, ctx, 0, keepdims=False)
        all_positions = lax.all_gather(positions, "ctx", axis=1, tiled=True)
        my_positions = lax.dynamic_index_in_dim(all_positions, ctx, 0, keepdims=False)
        angles = angles_for(my_positions, HD)
        gathered = gather_rows(mine)
        shape3 = gathered.shape
        flat_in = gathered.reshape(-1, width)
        raw = product(flat_in, full_qkv)
        raw_query, raw_key, raw_value = jnp.split(raw, 3, axis=1)

        def prepare_local(projected, gains):
            return prepare_heads(projected, angles, gains, HD)

        query_ready, query_back = jax.vjp(prepare_local, raw_query, sharpness)
        key_ready, key_back = jax.vjp(prepare_local, raw_key, sharpness)
        query_low = query_ready.astype(BF)
        key_low = key_ready.astype(BF)
        value_low = raw_value.astype(BF)
        attended, logsum = attend_both(query_low, key_low, value_low, ids)
        attend_sum = reduce_rows(product(attended, full_output).reshape(shape3))
        residual_float = mine.astype(F32)
        first, attend_back_mix = jax.vjp(branch_mix, attend_sum, residual_float, attend_rate)
        first_all = gather_rows(first.astype(BF)).reshape(-1, width)
        ug_raw = product(first_all, full_ug)
        up_raw, gate_raw = (ug_raw[:, :hidden_here], ug_raw[:, hidden_here:])
        hidden, activate_back = jax.vjp(activate, up_raw, gate_raw, amplitude, steepness)
        hidden_low = hidden.astype(BF)
        down_sum = reduce_rows(product(hidden_low, full_down).reshape(shape3))
        outcome, mixer_back = jax.vjp(branch_mix, down_sum, first, mixer_rate)
        layer_out = trade(outcome.astype(BF), sizes)
        my_cot = trade(cotangent, sizes)
        grad_down_sum, grad_first, grad_mixer_part = mixer_back(my_cot.astype(F32))
        down_grad_all = gather_rows(grad_down_sum.astype(BF)).reshape(-1, width)
        grad_hidden = transposed_right(down_grad_all, full_down)
        grad_down_part = transposed_left(hidden_low, down_grad_all)
        grad_up_raw, grad_gate_raw, grad_amplitude_part, grad_steepness_part = activate_back(
            grad_hidden
        )
        ug_grad = jnp.concatenate([grad_up_raw.astype(BF), grad_gate_raw.astype(BF)], axis=1)
        first_back = transposed_right(ug_grad, full_ug)
        grad_first = grad_first + reduce_rows(first_back.reshape(shape3))
        grad_ug_part = transposed_left(first_all, ug_grad)
        grad_attend_sum, grad_residual, grad_attend_part = attend_back_mix(grad_first)
        attend_grad_all = gather_rows(grad_attend_sum.astype(BF)).reshape(-1, width)
        grad_output_part = transposed_left(attended, attend_grad_all)
        grad_attended = transposed_right(attend_grad_all, full_output).astype(BF)
        grad_query_ready, grad_key_ready, grad_value_ready = attend_back(
            query_low, key_low, value_low, ids, logsum, grad_attended
        )
        grad_raw_query, sharp_query = query_back(grad_query_ready)
        grad_raw_key, sharp_key = key_back(grad_key_ready)
        qkv_grad = jnp.concatenate(
            [grad_raw_query.astype(BF), grad_raw_key.astype(BF), grad_value_ready.astype(BF)],
            axis=1,
        )
        input_back = transposed_right(qkv_grad, full_qkv)
        grad_input = grad_residual + reduce_rows(input_back.reshape(shape3))
        grad_input = trade(grad_input.astype(BF), sizes).astype(F32)
        grad_qkv_part = transposed_left(flat_in, qkv_grad)

        def sum_rows(part):
            share = lax.psum_scatter(
                part.astype(BF), ("fsdp", "ctx"), scatter_dimension=0, tiled=True
            )
            return lax.all_gather(share, "ctx", axis=0, tiled=True).astype(F32)

        def sum_columns(part):
            share = lax.psum_scatter(
                part.astype(BF), ("fsdp", "ctx"), scatter_dimension=1, tiled=True
            )
            return lax.all_gather(share, "ctx", axis=1, tiled=True).astype(F32)

        grad_down = sum_columns(grad_down_part)
        grad_ug = sum_rows(grad_ug_part)
        grad_output = sum_columns(grad_output_part)
        grad_qkv = sum_rows(grad_qkv_part)
        grad_up, grad_gate = (grad_ug[:, :hidden_here], grad_ug[:, hidden_here:])
        grad_query, grad_key, grad_value = jnp.split(grad_qkv, 3, axis=1)
        tensor_index = lax.axis_index("tp")
        tp = sizes["tp"]

        def spread_slice(section):
            return lax.dynamic_update_slice_in_dim(
                jnp.zeros((section.shape[0] * tp,), F32),
                section,
                tensor_index * section.shape[0],
                0,
            )

        grad_sharpness, grad_amplitude, grad_steepness, grad_attend, grad_mixer = lax.psum(
            (
                spread_slice(sharp_query + sharp_key),
                spread_slice(grad_amplitude_part),
                spread_slice(grad_steepness_part),
                grad_attend_part,
                grad_mixer_part,
            ),
            ("fsdp", "ctx", "tp"),
        )
        return (
            layer_out,
            grad_input,
            grad_query,
            grad_key,
            grad_value,
            grad_output,
            grad_sharpness,
            grad_attend,
            grad_up,
            grad_gate,
            grad_down,
            grad_amplitude,
            grad_steepness,
            grad_mixer,
        )

    return run


def solution(mesh):
    return jax.shard_map(
        per_device(dict(mesh.shape)),
        mesh=mesh,
        in_specs=(
            P("fsdp", ("ctx", "tp"), None),
            P("fsdp", "tp"),
            P("fsdp", "tp"),
            P("fsdp", "tp"),
            P("tp", "fsdp"),
            P("tp"),
            P(),
            P("fsdp", "tp"),
            P("fsdp", "tp"),
            P("tp", "fsdp"),
            P("tp"),
            P("tp"),
            P(),
            P("fsdp", None),
            P("fsdp", "ctx"),
            P("fsdp", ("ctx", "tp"), None),
        ),
        out_specs=(
            P("fsdp", ("ctx", "tp"), None),
            P("fsdp", ("ctx", "tp"), None),
            P("fsdp", "tp"),
            P("fsdp", "tp"),
            P("fsdp", "tp"),
            P("tp", "fsdp"),
            P(),
            P(),
            P("fsdp", "tp"),
            P("fsdp", "tp"),
            P("tp", "fsdp"),
            P(),
            P(),
            P(),
        ),
        check_vma=False,
    )
```

profile of v0, /device:TPU:0, one launch (start us, length us, event | category | flops | bytes accessed | tf_op | source)
XLA Modules:
  0.0 814.9 jit_solution(5183301861423763717)
XLA Ops:
  25.9 23.3 %all_gather.42 = bf16[256,1024]{1,0:T(8,128)(2,1)S(1)} all-gather(bf16[256,256]{1,0:T(8,128)(2,1)S(1)} %copy-done.32), channel_id=1, replica_groups=mesh['fsdp'=4,'ctx'=2,'tp'=4] {'fsdp'}, dimensions={1}, use_global_device_ids=true | all-gather | bytes 655360 | tf_op jit(solution)/shard_map/all_gather | solution.py:152
  58.4 23.6 %all-gather.9.cloned.1.call-done = bf16[2,512,1024]{2,1,0:T(8,128)(2,1)} async-done(((bf16[2,128,1024]{2,1,0:T(8,128)(2,1)}), bf16[2,512,1024]{2,1,0:T(8,128)(2,1)}) %all-gather.9.cloned.1.call-update) | async-done | bytes 2097168 | tf_op jit(solution)/shard_map/all_gather | solution.py:55
  95.2 8.0 fusion
  103.2 8.2 %fusion.14 = bf16[4,64,1024]{2,1,0:T(8,128)(2,1)} fusion(bf16[1024,4,64]{0,2,1:T(8,128)(2,1)S(1)} %bitcast.135, f32[4,1024,1024]{1,2,0:T(8,128)} %get-tuple-element.74, f32[4,1024]{1,0:T(4,128)S(1)} %fusion, f32[4,1024]{1,0:T(4,128)S(1)} %get-tuple-element.73), kind=kOutput, calls=%fused_computation.55 | convolution fusion | flops 549715968 | bytes 17858560 | tf_op jit(solution)/shard_map/hqk,khd->qhd/dot_general | solution.py:97
  117.5 28.8 %reduce-scatter.13.cloned.1.call-done = bf16[2,128,1024]{2,1,0:T(8,128)(2,1)} async-done(((bf16[2,512,1024]{2,1,0:T(8,128)(2,1)}), bf16[2,128,1024]{2,1,0:T(8,128)(2,1)}) %reduce-scatter.13.cloned.1.call-update) | async-done | bytes 524304 | tf_op jit(solution)/shard_map/reduce_scatter | solution.py:59
  152.5 76.5 %all-gather.15.cloned.1.call-done = bf16[1024,2048]{1,0:T(8,128)(2,1)} async-done(((bf16[256,2048]{1,0:T(8,128)(2,1)}), bf16[1024,2048]{1,0:T(8,128)(2,1)}) %all-gather.15.cloned.1.call-update) | async-done | bytes 4194320 | tf_op jit(solution)/shard_map/all_gather | solution.py:154
  229.0 23.1 %all-gather.13.cloned.1.call-done = bf16[2,512,1024]{2,1,0:T(8,128)(2,1)} async-done(((bf16[2,128,1024]{2,1,0:T(8,128)(2,1)}), bf16[2,512,1024]{2,1,0:T(8,128)(2,1)}) %all-gather.13.cloned.1.call-update) | async-done | bytes 2097168 | tf_op jit(solution)/shard_map/all_gather | solution.py:55
  264.7 35.1 %all-gather.17.cloned.1.call-done = bf16[1024,1024]{1,0:T(8,128)(2,1)} async-done(((bf16[1024,256]{1,0:T(8,128)(2,1)}), bf16[1024,1024]{1,0:T(8,128)(2,1)}) %all-gather.17.cloned.1.call-update) | async-done | bytes 2097168 | tf_op jit(solution)/shard_map/all_gather | solution.py:155
  314.7 20.5 %reduce-scatter.15.cloned.1.call-done = bf16[2,128,1024]{2,1,0:T(8,128)(2,1)} async-done(((bf16[2,512,1024]{2,1,0:T(8,128)(2,1)}), bf16[2,128,1024]{2,1,0:T(8,128)(2,1)}) %reduce-scatter.15.cloned.1.call-update) | async-done | bytes 524304 | tf_op jit(solution)/shard_map/reduce_scatter | solution.py:59
  343.0 22.4 %all-gather.19.cloned.1.call-done = bf16[2,512,1024]{2,1,0:T(8,128)(2,1)} async-done(((bf16[2,128,1024]{2,1,0:T(8,128)(2,1)}), bf16[2,512,1024]{2,1,0:T(8,128)(2,1)}) %all-gather.19.cloned.1.call-update) | async-done | bytes 2097168 | tf_op jit(solution)/shard_map/all_gather | solution.py:55
  365.5 9.4 %multiply_reduce_fusion.1 = (f32[1024]{0:T(1024)}, f32[1024]{0:T(1024)}, f32[1024,1024]{1,0:T(8,128)S(1)}, bf16[1024,1024]{1,0:T(8,128)(2,1)S(1)}) fusion(f32[1024,2048]{1,0:T(8,128)} %copy-done.9, f32[1024]{0:T(1024)} %param.27, f32[1024]{0:T(1024)} %param.26, bf16[1024,1024]{1,0:T(8,128)(2,1)} %bitcast.157, ...), kind=kOutput, calls=%fused_computation.15 | convolution fusion | flops 2168453120 | bytes 18890752 | tf_op jit(solution)/shard_map/dot_general | solution.py:51
  384.4 31.3 %reduce-scatter.17.cloned.1.call-done = bf16[2,128,1024]{2,1,0:T(8,128)(2,1)} async-done(((bf16[2,512,1024]{2,1,0:T(8,128)(2,1)}), bf16[2,128,1024]{2,1,0:T(8,128)(2,1)}) %reduce-scatter.17.cloned.1.call-update) | async-done | bytes 524304 | tf_op jit(solution)/shard_map/reduce_scatter | solution.py:59
  424.0 9.4 %convolution_convert_fusion = bf16[1024,2048]{1,0:T(8,128)(2,1)} fusion(bf16[1024,1024]{1,0:T(8,128)(2,1)} %bitcast.156, bf16[1024,1024]{1,0:T(8,128)(2,1)} %copy-done.18, bf16[1024,1024]{1,0:T(8,128)(2,1)} %copy-done.59), kind=kOutput, calls=%fused_computation.24 | convolution fusion | flops 4305453056 | bytes 10485760 | tf_op jit(solution)/shard_map/dot_general | solution.py:47
  452.2 13.7 %multiply_reduce_fusion = (f32[4,1024]{1,0:T(4,128)S(1)}, f32[4,1024,1024]{1,2,0:T(8,128)}) fusion(f32[4,1024,1024]{1,2,0:T(8,128)} %get-tuple-element.74, f32[4,1024]{1,0:T(4,128)S(1)} %log_add_fusion, bf16[1024,4,64]{0,2,1:T(8,128)(2,1)S(1)} %bitcast.133, bf16[1024,4,64]{0,2,1:T(8,128)(2,1)} %bitcast.136), kind=kOutput, calls=%fused_computation.1 | convolution fusion | flops 549449728 | bytes 34635776 | tf_op jit(solution)/shard_map/qhd,khd->hqk/dot_general | solution.py:113
  469.5 10.9 %multiply_convert_fusion = bf16[4,1024,1024]{1,2,0:T(8,128)(2,1)} fusion(f32[4,1024,1024]{1,2,0:T(8,128)} %get-tuple-element.76, f32[4,1024,1024]{1,2,0:T(8,128)S(1)} %bitcast.129, f32[4,1024]{1,0:T(4,128)S(1)} %get-tuple-element.75, f32[4,1024]{1,0:T(4,128)S(1)} %log_add_fusion), kind=kLoop, calls=%fused_computation | loop fusion | flops 16777216 | bytes 41975808 | tf_op jit(solution)/shard_map/convert_element_type | solution.py:115
  492.5 46.2 %reduce-scatter.23.cloned.1.call-done = bf16[128,2048]{1,0:T(8,128)(2,1)} async-done(((bf16[1024,2048]{1,0:T(8,128)(2,1)}), bf16[128,2048]{1,0:T(8,128)(2,1)}) %reduce-scatter.23.cloned.1.call-update) | async-done | bytes 524304 | tf_op jit(solution)/shard_map/reduce_scatter | solution.py:218
  538.9 8.6 %fusion.11 = bf16[4,64,1024]{2,1,0:T(8,128)(2,1)S(1)} fusion(bf16[1024,4,64]{0,2,1:T(8,128)(2,1)S(1)} %bitcast.134, f32[4,1024,1024]{1,2,0:T(8,128)} %get-tuple-element.74, f32[4,1024]{1,0:T(4,128)S(1)} %log_add_fusion), kind=kOutput, calls=%fused_computation.52 | convolution fusion | flops 545521664 | bytes 17842176 | tf_op jit(solution)/shard_map/hqk,qhd->khd/dot_general | solution.py:112
  557.1 8.3 %collective-permute-done.1 = bf16[128,1024]{1,0:T(8,128)(2,1)S(1)} collective-permute-done((bf16[128,1024]{1,0:T(8,128)(2,1)S(1)}, bf16[128,1024]{1,0:T(8,128)(2,1)S(1)}, u32[]{:S(2)}, u32[]{:S(2)}) %collective-permute-start.1) | collective-permute-done | bytes 262176 | tf_op jit(solution)/shard_map/ppermute | solution.py:77
  566.8 43.6 %reduce-scatter.27.cloned.1.call-done = bf16[128,1024]{1,0:T(8,128)(2,1)} async-done(((bf16[1024,1024]{1,0:T(8,128)(2,1)}), bf16[128,1024]{1,0:T(8,128)(2,1)}) %reduce-scatter.27.cloned.1.call-update) | async-done | bytes 262160
  620.1 40.8 %all-reduce.4 = (f32[1024]{0:T(1024)}, f32[1024]{0:T(1024)}, f32[4096]{0:T(1024)}, f32[4096]{0:T(1024)}, f32[1024]{0:T(1024)}) all-reduce(f32[1024]{0:T(1024)S(1)} %dynamic_update_slice.9, f32[1024]{0:T(1024)S(1)} %copy-done.44, f32[4096]{0:T(1024)S(1)} %dynamic_update_slice.10, ...), channel_id=1, replica_groups=mesh['fsdp'=4,'ctx'=2,'tp'=4] {'fsdp','ctx','tp'}, use_global_device_ids=true, to_apply=%region_23.24 | all-reduce | flops 11264 | bytes 90112 | tf_op jit(solution)/shard_map/psum | solution.py:246
  660.8 14.6 %reduce-scatter.25.cloned.1.call-done = bf16[128,256]{1,0:T(8,128)(2,1)} async-done(((bf16[1024,256]{1,0:T(8,128)(2,1)}), bf16[128,256]{1,0:T(8,128)(2,1)}) %reduce-scatter.25.cloned.1.call-update) | async-done | bytes 65552
  682.1 15.1 %all-gather.23.cloned.1.call-done = bf16[256,2048]{1,0:T(8,128)(2,1)} async-done(((bf16[128,2048]{1,0:T(8,128)(2,1)}), bf16[256,2048]{1,0:T(8,128)(2,1)}) %all-gather.23.cloned.1.call-update) | async-done | bytes 1048592 | tf_op jit(solution)/shard_map/all_gather | solution.py:221
  700.0 30.8 %reduce-scatter.19.cloned.1.call-done = bf16[2,128,1024]{2,1,0:T(8,128)(2,1)} async-done(((bf16[2,512,1024]{2,1,0:T(8,128)(2,1)}), bf16[2,128,1024]{2,1,0:T(8,128)(2,1)}) %reduce-scatter.19.cloned.1.call-update) | async-done | bytes 524304 | tf_op jit(solution)/shard_map/reduce_scatter | solution.py:59
  733.6 66.1 %reduce-scatter.21.cloned.1.call-done = bf16[128,768]{1,0:T(8,128)(2,1)} async-done(((bf16[1024,768]{1,0:T(8,128)(2,1)}), bf16[128,768]{1,0:T(8,128)(2,1)}) %reduce-scatter.21.cloned.1.call-update) | async-done | bytes 196624 | tf_op jit(solution)/shard_map/reduce_scatter | solution.py:218
  (257 shorter events, 181.8 us)
Async XLA Ops:
  7.2 51.2 %all-gather.11.cloned.1.call-start = ((), (), s32[]{:S(2)}) async-start(), calls=%async_computation.9 | async-start | bytes 1966080 | tf_op jit(solution)/shard_map/all_gather | solution.py:151
  9.1 72.9 %all-gather.9.cloned.1.call-start = ((), (), s32[]{:S(2)}) async-start(), calls=%async_computation.8 | async-start | bytes 2621440 | tf_op jit(solution)/shard_map/all_gather | solution.py:55
  10.2 9.3 %collective-permute-start = (bf16[128,1024]{1,0:T(8,128)(2,1)S(1)}, bf16[128,1024]{1,0:T(8,128)(2,1)S(1)}, u32[]{:S(2)}, u32[]{:S(2)}) collective-permute-start(bf16[128,1024]{1,0:T(8,128)(2,1)S(1)} %dynamic-slice_bitcast_fusion.3), channel_id=1, source_target_pairs={{0,4},{4,0},{1,5},{5,1},{2,6},{6,2},{3,7},{7,3},{8,12},{12,8},{9,1... | collective-permute-start | bytes 786440 | tf_op jit(solution)/shard_map/ppermute | solution.py:77
  20.5 316.0 %copy-start.5 = (bf16[1,128,1024]{2,1,0:T(8,128)(2,1)}, bf16[1,128,1024]{2,1,0:T(8,128)(2,1)S(1)}, u32[]{:S(2)}) copy-start(bf16[1,128,1024]{2,1,0:T(8,128)(2,1)S(1)} %get-tuple-element.55) | copy-start | bytes 786436
  21.4 124.8 %reduce-scatter.13.cloned.1.call-start = ((), (), s32[]{:S(2)}) async-start(), calls=%async_computation.10 | async-start | bytes 2621440 | tf_op jit(solution)/shard_map/reduce_scatter | solution.py:59
  114.9 114.1 %all-gather.15.cloned.1.call-start = ((), (), s32[]{:S(2)}) async-start(), calls=%async_computation.12 | async-start | bytes 5242880 | tf_op jit(solution)/shard_map/all_gather | solution.py:154
  117.2 134.8 %all-gather.13.cloned.1.call-start = ((), (), s32[]{:S(2)}) async-start(), calls=%async_computation.11 | async-start | bytes 2621440 | tf_op jit(solution)/shard_map/all_gather | solution.py:55
  148.1 111.0 %copy-start.39 = (f32[2,128]{1,0:T(2,128)}, f32[2,128]{1,0:T(2,128)S(1)}, u32[]{:S(2)}) copy-start(f32[2,128]{1,0:T(2,128)S(1)} %fusion.39) | copy-start | bytes 3076
  151.9 147.9 %all-gather.17.cloned.1.call-start = ((), (), s32[]{:S(2)}) async-start(), calls=%async_computation.13 | async-start | bytes 2621440 | tf_op jit(solution)/shard_map/all_gather | solution.py:155
  152.5 182.8 %reduce-scatter.15.cloned.1.call-start = ((), (), s32[]{:S(2)}) async-start(), calls=%async_computation.14 | async-start | bytes 2621440 | tf_op jit(solution)/shard_map/reduce_scatter | solution.py:59
  305.7 59.8 %all-gather.19.cloned.1.call-start = ((), (), s32[]{:S(2)}) async-start(), calls=%async_computation.15 | async-start | bytes 2621440 | tf_op jit(solution)/shard_map/all_gather | solution.py:55
  305.8 7.9 collective-permute-start.2
  342.8 72.9 %reduce-scatter.17.cloned.1.call-start = ((), (), s32[]{:S(2)}) async-start(), calls=%async_computation.16 | async-start | bytes 2621440 | tf_op jit(solution)/shard_map/reduce_scatter | solution.py:59
  384.4 62.3 %all-gather.21.cloned.1.call-start = ((), (), s32[]{:S(2)}) async-start(), calls=%async_computation.17 | async-start | bytes 2621440 | tf_op jit(solution)/shard_map/all_gather | solution.py:55
  424.0 114.7 %reduce-scatter.23.cloned.1.call-start = ((), (), s32[]{:S(2)}) async-start(), calls=%async_computation.20 | async-start | bytes 4718592 | tf_op jit(solution)/shard_map/reduce_scatter | solution.py:218
  433.5 176.9 %reduce-scatter.27.cloned.1.call-start = ((), (), s32[]{:S(2)}) async-start(), calls=%async_computation.23 | async-start | bytes 2359296
  444.2 231.3 %reduce-scatter.25.cloned.1.call-start = ((), (), s32[]{:S(2)}) async-start(), calls=%async_computation.22 | async-start | bytes 589824
  489.8 207.4 %all-gather.23.cloned.1.call-start = ((), (), s32[]{:S(2)}) async-start(), calls=%async_computation.21 | async-start | bytes 1572864 | tf_op jit(solution)/shard_map/all_gather | solution.py:221
  538.7 192.1 %reduce-scatter.19.cloned.1.call-start = ((), (), s32[]{:S(2)}) async-start(), calls=%async_computation.18 | async-start | bytes 2621440 | tf_op jit(solution)/shard_map/reduce_scatter | solution.py:59
  550.7 248.9 %reduce-scatter.21.cloned.1.call-start = ((), (), s32[]{:S(2)}) async-start(), calls=%async_computation.19 | async-start | bytes 1769472 | tf_op jit(solution)/shard_map/reduce_scatter | solution.py:218
  555.5 9.8 %collective-permute-start.1 = (bf16[128,1024]{1,0:T(8,128)(2,1)S(1)}, bf16[128,1024]{1,0:T(8,128)(2,1)S(1)}, u32[]{:S(2)}, u32[]{:S(2)}) collective-permute-start(bf16[128,1024]{1,0:T(8,128)(2,1)S(1)} %dynamic-slice_bitcast_fusion.2), channel_id=1, source_target_pairs={{0,4},{4,0},{1,5},{5,1},{2,6},{6,2},{3,7},{7,3},{8,12},{12,8},{9,1... | collective-permute-start | bytes 786440 | tf_op jit(solution)/shard_map/ppermute | solution.py:77
  566.2 164.6 %copy-start.7 = (f32[2,128,1024]{2,1,0:T(8,128)S(1)}, f32[2,128,1024]{2,1,0:T(8,128)}, u32[]{:S(2)}) copy-start(f32[2,128,1024]{2,1,0:T(8,128)} %copy-done.6) | copy-start | bytes 3145732
  566.2 164.6 %copy-start.27 = (f32[1024]{0:T(1024)S(1)}, f32[1024]{0:T(1024)}, u32[]{:S(2)}) copy-start(f32[1024]{0:T(1024)} %param.22) | copy-start | bytes 12292
  732.1 75.1 %collective-permute-start.3 = (bf16[128,1024]{1,0:T(8,128)(2,1)S(1)}, bf16[128,1024]{1,0:T(8,128)(2,1)S(1)}, u32[]{:S(2)}, u32[]{:S(2)}) collective-permute-start(bf16[128,1024]{1,0:T(8,128)(2,1)S(1)} %dynamic-slice_bitcast_fusion), channel_id=1, source_target_pairs={{0,4},{4,0},{1,5},{5,1},{2,6},{6,2},{3,7},{7,3},{8,12},{12,8},{9,1... | collective-permute-start | bytes 786440 | tf_op jit(solution)/shard_map/ppermute | solution.py:77
  (60 other events, 1082.7 us)
Sparse Core Ops, SparseCore 0:
  10.2 48.1 all-gather.10
  60.5 21.4 all-gather.8
  115.0 31.1 reduce-scatter.12
  148.2 80.7 all-gather.14
  231.0 21.0 all-gather.12
  253.5 46.2 all-gather.16
  305.8 29.3 reduce-scatter.14
  342.9 22.5 all-gather.18
  384.5 31.1 reduce-scatter.16
  424.1 22.5 all-gather.20
  450.3 88.2 reduce-scatter.22
  542.1 68.3 reduce-scatter.26
  613.8 61.6 reduce-scatter.24
  676.8 20.3 all-gather.22
  699.6 31.1 reduce-scatter.18
  734.1 65.5 reduce-scatter.20
where the time goes:
time: 824 us; the launch traced here: 815 us
  waiting for transfers between devices  509 us (62%)
  matrix products  109 us (13%)
  blocking collectives  87.1 us (11%)
  other arithmetic  58.8 us (7%)
  local copies, waits for them, and re-layouts  26.9 us (3%)
  between operations  14.9 us (2%)
  starting transfers between devices  9.26 us (1%)
    reduce_scatter x2, waiting for transfers between devices, sum_rows(): lax.psum_scatter(part.astype(BF), ('fsdp', 'ctx'), scatter_dimension=0, t...  112 us
    reduce_scatter x4, waiting for transfers between devices, reduce_rows(): lax.psum_scatter(values.astype(BF), 'tp', scatter_dimension=1, tiled=True)  111 us
    all_gather x1, waiting for transfers between devices, run(): full_ug = lax.all_gather(ug_shard, 'fsdp', axis=0, tiled=True)  76.5 us
    all_gather x4, waiting for transfers between devices, gather_rows(): return lax.all_gather(values, 'tp', axis=1, tiled=True)  71.6 us
    unnamed x18, waiting for transfers between devices  59 us
    psum x1, blocking collectives, run(): lax.psum((spread_slice(sharp_query + sharp_key), spread_slice(grad_amplit...  40.8 us
    all_gather x1, waiting for transfers between devices, run(): full_down = lax.all_gather(down_weight, 'fsdp', axis=1, tiled=True)  35.1 us
    all_gather x1, blocking collectives, run(): full_output = lax.all_gather(output_weight, 'fsdp', axis=1, tiled=True)  23.3 us
  transfers between devices with their start and end apart: 20, of which 19 were waited for; matrix products, arithmetic and copies ran while one was open for 14% of the time, Pallas kernels for 0%

commit v1 on v0

--- a/solution.py
+++ b/solution.py
@@ -9,6 +9,19 @@
 rope_base = 10000.0
 BF = jnp.bfloat16
 F32 = jnp.float32
+
+
+def ring_gather(value, axis, dim):
+    ways = lax.axis_size(axis)
+    up = [(d, (d + 1) % ways) for d in range(ways)]
+    down = [(d, (d - 1) % ways) for d in range(ways)]
+    earlier, later = ([value], [value])
+    for _ in range(ways // 2):
+        earlier.append(lax.ppermute(earlier[-1], axis, up))
+    for _ in range((ways - 1) // 2):
+        later.append(lax.ppermute(later[-1], axis, down))
+    line = jnp.concatenate([*earlier[::-1], *later[1:]], axis=dim)
+    return jnp.roll(line, (lax.axis_index(axis) - ways // 2) * value.shape[dim], axis=dim)
 
 
 def unit_rows(values):
@@ -52,7 +65,7 @@
 
 
 def gather_rows(values):
-    return lax.all_gather(values, "tp", axis=1, tiled=True)
+    return ring_gather(values, "tp", 1)
 
 
 def reduce_rows(values):

time: 824 us -> 757 us (0.919)
  waiting for transfers between devices: 509 us -> 422 us
  other arithmetic: 58.8 us -> 88.6 us
  matrix products: 109 us -> 97.1 us
    all_gather x4 -> x0, waiting for transfers between devices: 71.6 us -> none  [gather_rows(): return lax.all_gather(values, 'tp', axis=1, tiled=True)]
    ppermute x0 -> x12, waiting for transfers between devices: none -> 65.1 us  [the longest x8 55.1 us: ring_gather(): earlier.append(lax.ppermute(earlier[-1], axis, up))]
    reduce_scatter x2, waiting for transfers between devices: 112 us -> 63.9 us  [sum_rows(): lax.psum_scatter(part.astype(BF), ('fsdp', 'ctx'), scatter_dimension=0, t...]
    concatenate x0 -> x4, other arithmetic: none -> 33.6 us  [ring_gather(): jnp.roll(line, (lax.axis_index(axis) - ways // 2) * value.shape[dim], axi...]
    all_gather x1, waiting for transfers between devices: 76.5 us -> 46.6 us  [run(): full_ug = lax.all_gather(ug_shard, 'fsdp', axis=0, tiled=True)]
    unnamed x18 -> x14, waiting for transfers between devices: 59 us -> 81.7 us
    reduce_scatter x4, waiting for transfers between devices: 111 us -> 96.9 us  [reduce_rows(): lax.psum_scatter(values.astype(BF), 'tp', scatter_dimension=1, tiled=True)]
    unnamed x132 -> x134, local copies, waits for them, and re-layouts: 19.6 us -> 15.5 us
  transfers between devices with their start and end apart: 20 -> 28, of which waited for: 19 -> 22; matrix products, arithmetic and copies ran while one was open for 14% -> 17% of each run, Pallas kernels for 0% -> 0%
where the time goes in v1:
time: 757 us; the launch traced here: 747 us
  waiting for transfers between devices  422 us (56%)
  matrix products  97.1 us (13%)
  other arithmetic  88.6 us (12%)
  blocking collectives  87.4 us (12%)
  local copies, waits for them, and re-layouts  21.7 us (3%)
  between operations  15.4 us (2%)
  starting transfers between devices  15 us (2%)
    reduce_scatter x4, waiting for transfers between devices, reduce_rows(): lax.psum_scatter(values.astype(BF), 'tp', scatter_dimension=1, tiled=True)  96.9 us
    unnamed x14, waiting for transfers between devices  81.7 us
    reduce_scatter x2, waiting for transfers between devices, sum_rows(): lax.psum_scatter(part.astype(BF), ('fsdp', 'ctx'), scatter_dimension=0, t...  63.9 us
    ppermute x8, waiting for transfers between devices, ring_gather(): earlier.append(lax.ppermute(earlier[-1], axis, up))  55.1 us
    all_gather x1, waiting for transfers between devices, run(): full_ug = lax.all_gather(ug_shard, 'fsdp', axis=0, tiled=True)  46.6 us
    psum x1, blocking collectives, run(): lax.psum((spread_slice(sharp_query + sharp_key), spread_slice(grad_amplit...  40.7 us
    concatenate x4, other arithmetic, ring_gather(): jnp.roll(line, (lax.axis_index(axis) - ways // 2) * value.shape[dim], axi...  33.6 us
    all_gather x1, waiting for transfers between devices, run(): full_down = lax.all_gather(down_weight, 'fsdp', axis=1, tiled=True)  33.6 us
  transfers between devices with their start and end apart: 28, of which 22 were waited for; matrix products, arithmetic and copies ran while one was open for 17% of the time, Pallas kernels for 0%

profile of v1, /device:TPU:0, one launch (start us, length us, event | category | flops | bytes accessed | tf_op | source)
XLA Modules:
  0.0 746.8 jit_solution(10174493325256648285)
XLA Ops:
  24.6 23.5 %all_gather.29 = bf16[256,1024]{1,0:T(8,128)(2,1)S(1)} all-gather(bf16[256,256]{1,0:T(8,128)(2,1)} %param.22), channel_id=1, replica_groups=mesh['fsdp'=4,'ctx'=2,'tp'=4] {'fsdp'}, dimensions={1}, use_global_device_ids=true | all-gather | bytes 655360 | tf_op jit(solution)/shard_map/all_gather | solution.py:165
  49.9 10.1 %collective-permute-done.3 = bf16[2,128,1024]{2,1,0:T(8,128)(2,1)S(1)} collective-permute-done((bf16[2,128,1024]{2,1,0:T(8,128)(2,1)}, bf16[2,128,1024]{2,1,0:T(8,128)(2,1)S(1)}, u32[]{:S(2)}, u32[]{:S(2)}) %collective-permute-start.3) | collective-permute-done | bytes 524320 | tf_op jit(solution)/shard_map/ppermute | solution.py:22
  103.9 29.3 %reduce-scatter.13.cloned.1.call-done = bf16[2,128,1024]{2,1,0:T(8,128)(2,1)} async-done(((bf16[2,512,1024]{2,1,0:T(8,128)(2,1)}), bf16[2,128,1024]{2,1,0:T(8,128)(2,1)}) %reduce-scatter.13.cloned.1.call-update) | async-done | bytes 524304 | tf_op jit(solution)/shard_map/reduce_scatter | solution.py:72
  140.0 11.6 %collective-permute-done.4 = bf16[2,128,1024]{2,1,0:T(8,128)(2,1)S(1)} collective-permute-done((bf16[2,128,1024]{2,1,0:T(8,128)(2,1)S(1)}, bf16[2,128,1024]{2,1,0:T(8,128)(2,1)S(1)}, u32[]{:S(2)}, u32[]{:S(2)}) %collective-permute-start.4) | collective-permute-done | bytes 524320 | tf_op jit(solution)/shard_map/ppermute | solution.py:20
  151.6 8.6 %collective-permute-done.5 = bf16[2,128,1024]{2,1,0:T(8,128)(2,1)S(1)} collective-permute-done((bf16[2,128,1024]{2,1,0:T(8,128)(2,1)S(1)}, bf16[2,128,1024]{2,1,0:T(8,128)(2,1)S(1)}, u32[]{:S(2)}, u32[]{:S(2)}) %collective-permute-start.5) | collective-permute-done | bytes 524320 | tf_op jit(solution)/shard_map/ppermute | solution.py:20
  160.2 9.4 %fusion.27 = bf16[2,512,1024]{2,1,0:T(8,128)(2,1)} fusion(s32[]{:T(128)S(6)} %select_n.95, bf16[2,128,1024]{2,1,0:T(8,128)(2,1)S(1)} %collective-permute-done.5, bf16[2,128,1024]{2,1,0:T(8,128)(2,1)S(1)} %collective-permute-done.4, bf16[2,128,1024]{2,1,0:T(8,128)(2,1)S(1)} %multiply_convert_fusion.7, bf16[2,128,1024]{2,1,0:T(8,128)(2,1)S(1)} %collective-permute-done.6), kind=kLoop, calls=%fused_computation.77 | loop fusion | flops 16777216 | bytes 4194308 | tf_op jit(solution)/shard_map/jit(_roll_dynamic)/concatenate | solution.py:24
  169.5 46.6 %all-gather.7.cloned.1.call-done = bf16[1024,2048]{1,0:T(8,128)(2,1)} async-done(((bf16[256,2048]{1,0:T(8,128)(2,1)}), bf16[1024,2048]{1,0:T(8,128)(2,1)}) %all-gather.7.cloned.1.call-update) | async-done | bytes 4194320 | tf_op jit(solution)/shard_map/all_gather | solution.py:167
  228.8 33.6 %all-gather.9.cloned.1.call-done = bf16[1024,1024]{1,0:T(8,128)(2,1)} async-done(((bf16[1024,256]{1,0:T(8,128)(2,1)}), bf16[1024,1024]{1,0:T(8,128)(2,1)}) %all-gather.9.cloned.1.call-update) | async-done | bytes 2097168 | tf_op jit(solution)/shard_map/all_gather | solution.py:168
  276.5 21.3 %reduce-scatter.15.cloned.1.call-done = bf16[2,128,1024]{2,1,0:T(8,128)(2,1)} async-done(((bf16[2,512,1024]{2,1,0:T(8,128)(2,1)}), bf16[2,128,1024]{2,1,0:T(8,128)(2,1)}) %reduce-scatter.15.cloned.1.call-update) | async-done | bytes 524304 | tf_op jit(solution)/shard_map/reduce_scatter | solution.py:72
  306.4 11.9 %collective-permute-done.9 = bf16[2,128,1024]{2,1,0:T(8,128)(2,1)S(1)} collective-permute-done((bf16[2,128,1024]{2,1,0:T(8,128)(2,1)S(1)}, bf16[2,128,1024]{2,1,0:T(8,128)(2,1)S(1)}, u32[]{:S(2)}, u32[]{:S(2)}) %collective-permute-start.9) | collective-permute-done | bytes 524320 | tf_op jit(solution)/shard_map/ppermute | solution.py:20
  318.3 8.6 %collective-permute-done.10 = bf16[2,128,1024]{2,1,0:T(8,128)(2,1)S(1)} collective-permute-done((bf16[2,128,1024]{2,1,0:T(8,128)(2,1)S(1)}, bf16[2,128,1024]{2,1,0:T(8,128)(2,1)S(1)}, u32[]{:S(2)}, u32[]{:S(2)}) %collective-permute-start.10) | collective-permute-done | bytes 524320 | tf_op jit(solution)/shard_map/ppermute | solution.py:20
  335.4 8.5 %multiply_reduce_fusion.1 = (f32[1024]{0:T(1024)}, f32[1024]{0:T(1024)}, f32[1024,1024]{1,0:T(8,128)S(1)}, bf16[1024,1024]{1,0:T(8,128)(2,1)S(1)}) fusion(f32[1024,2048]{1,0:T(8,128)} %copy-done.8, f32[1024]{0:T(1024)S(1)} %copy-done.50, f32[1024]{0:T(1024)S(1)} %copy-done.58, bf16[1024,1024]{1,0:T(8,128)(2,1)S(1)} %bitcast.140, ...), kind=kOutput, calls=%fused_computation.49 | convolution fusion | flops 2168453120 | bytes 18890752 | tf_op jit(solution)/shard_map/dot_general | solution.py:64
  353.6 9.5 %convolution_convert_fusion = bf16[1024,2048]{1,0:T(8,128)(2,1)} fusion(bf16[1024,1024]{1,0:T(8,128)(2,1)} %bitcast.139, bf16[1024,1024]{1,0:T(8,128)(2,1)} %copy-done.21, bf16[1024,1024]{1,0:T(8,128)(2,1)} %copy-done.64), kind=kOutput, calls=%fused_computation.58 | convolution fusion | flops 4305453056 | bytes 10485760 | tf_op jit(solution)/shard_map/dot_general | solution.py:60
  363.2 21.2 %reduce-scatter.17.cloned.1.call-done = bf16[2,128,1024]{2,1,0:T(8,128)(2,1)} async-done(((bf16[2,512,1024]{2,1,0:T(8,128)(2,1)}), bf16[2,128,1024]{2,1,0:T(8,128)(2,1)}) %reduce-scatter.17.cloned.1.call-update) | async-done | bytes 524304 | tf_op jit(solution)/shard_map/reduce_scatter | solution.py:72
  392.1 11.7 %collective-permute-done.12 = bf16[2,128,1024]{2,1,0:T(8,128)(2,1)S(1)} collective-permute-done((bf16[2,128,1024]{2,1,0:T(8,128)(2,1)S(1)}, bf16[2,128,1024]{2,1,0:T(8,128)(2,1)S(1)}, u32[]{:S(2)}, u32[]{:S(2)}) %collective-permute-start.12) | collective-permute-done | bytes 524320 | tf_op jit(solution)/shard_map/ppermute | solution.py:20
  420.8 11.1 %multiply_reduce_fusion = (f32[4,1024]{1,0:T(4,128)S(1)}, f32[4,1024,1024]{1,2,0:T(8,128)}) fusion(f32[4,1024,1024]{1,2,0:T(8,128)} %get-tuple-element.75, f32[4,1024]{1,0:T(4,128)S(1)} %log_add_fusion, bf16[1024,4,64]{0,2,1:T(8,128)(2,1)S(1)} %bitcast.131, bf16[1024,4,64]{0,2,1:T(8,128)(2,1)S(1)} %bitcast.134), kind=kOutput, calls=%fused_computation.1 | convolution fusion | flops 549449728 | bytes 34635776 | tf_op jit(solution)/shard_map/qhd,khd->hqk/dot_general | solution.py:126
  433.7 12.3 %multiply_convert_fusion = bf16[4,1024,1024]{1,2,0:T(8,128)(2,1)S(1)} fusion(f32[4,1024,1024]{1,2,0:T(8,128)} %get-tuple-element.77, f32[4,1024,1024]{1,2,0:T(8,128)} %get-tuple-element.75, f32[4,1024]{1,0:T(4,128)S(1)} %get-tuple-element.76, f32[4,1024]{1,0:T(4,128)S(1)} %log_add_fusion), kind=kLoop, calls=%fused_computation | loop fusion | flops 16777216 | bytes 41975808 | tf_op jit(solution)/shard_map/convert_element_type | solution.py:128
  455.5 8.7 %fusion.41 = bf16[4,64,1024]{2,1,0:T(8,128)(2,1)S(1)} fusion(bf16[1024,4,64]{0,2,1:T(8,128)(2,1)S(1)} %bitcast.132, f32[4,1024,1024]{1,2,0:T(8,128)} %get-tuple-element.75, f32[4,1024]{1,0:T(4,128)S(1)} %log_add_fusion), kind=kOutput, calls=%fused_computation.116 | convolution fusion | flops 545521664 | bytes 17842176 | tf_op jit(solution)/shard_map/hqk,qhd->khd/dot_general | solution.py:125
  480.9 66.9 %reduce-scatter.27.cloned.1.call-done = bf16[128,1024]{1,0:T(8,128)(2,1)} async-done(((bf16[1024,1024]{1,0:T(8,128)(2,1)}), bf16[128,1024]{1,0:T(8,128)(2,1)}) %reduce-scatter.27.cloned.1.call-update) | async-done | bytes 262160
  557.6 40.7 %all-reduce.4 = (f32[1024]{0:T(1024)}, f32[1024]{0:T(1024)}, f32[4096]{0:T(1024)}, f32[4096]{0:T(1024)}, f32[1024]{0:T(1024)}) all-reduce(f32[1024]{0:T(1024)S(1)} %dynamic_update_slice.9, f32[1024]{0:T(1024)S(1)} %copy-done.48, f32[4096]{0:T(1024)S(1)} %dynamic_update_slice.10, ...), channel_id=1, replica_groups=mesh['fsdp'=4,'ctx'=2,'tp'=4] {'fsdp','ctx','tp'}, use_global_device_ids=true, to_apply=%region_23.25 | all-reduce | flops 11264 | bytes 90112 | tf_op jit(solution)/shard_map/psum | solution.py:259
  598.2 14.6 %reduce-scatter.25.cloned.1.call-done = bf16[128,256]{1,0:T(8,128)(2,1)} async-done(((bf16[1024,256]{1,0:T(8,128)(2,1)}), bf16[128,256]{1,0:T(8,128)(2,1)}) %reduce-scatter.25.cloned.1.call-update) | async-done | bytes 65552
  619.5 61.2 %reduce-scatter.21.cloned.1.call-done = bf16[128,768]{1,0:T(8,128)(2,1)} async-done(((bf16[1024,768]{1,0:T(8,128)(2,1)}), bf16[128,768]{1,0:T(8,128)(2,1)}) %reduce-scatter.21.cloned.1.call-update) | async-done | bytes 196624 | tf_op jit(solution)/shard_map/reduce_scatter | solution.py:231
  688.1 25.1 %reduce-scatter.19.cloned.1.call-done = bf16[2,128,1024]{2,1,0:T(8,128)(2,1)} async-done(((bf16[2,512,1024]{2,1,0:T(8,128)(2,1)}), bf16[2,128,1024]{2,1,0:T(8,128)(2,1)}) %reduce-scatter.19.cloned.1.call-update) | async-done | bytes 524304 | tf_op jit(solution)/shard_map/reduce_scatter | solution.py:72
  716.0 19.9 %all-gather.11.cloned.1.call-done = bf16[256,2048]{1,0:T(8,128)(2,1)} async-done(((bf16[128,2048]{1,0:T(8,128)(2,1)}), bf16[256,2048]{1,0:T(8,128)(2,1)}) %all-gather.11.cloned.1.call-update) | async-done | bytes 1048592 | tf_op jit(solution)/shard_map/all_gather | solution.py:234
  (274 shorter events, 205.7 us)
Async XLA Ops:
  7.2 63.4 %all-gather.5.cloned.1.call-start = ((), (), s32[]{:S(2)}) async-start(), calls=%async_computation.8 | async-start | bytes 1966080 | tf_op jit(solution)/shard_map/all_gather | solution.py:164
  8.2 9.3 %collective-permute-start = (bf16[128,1024]{1,0:T(8,128)(2,1)S(1)}, bf16[128,1024]{1,0:T(8,128)(2,1)S(1)}, u32[]{:S(2)}, u32[]{:S(2)}) collective-permute-start(bf16[128,1024]{1,0:T(8,128)(2,1)S(1)} %dynamic-slice_bitcast_fusion.3), channel_id=1, source_target_pairs={{0,4},{4,0},{1,5},{5,1},{2,6},{6,2},{3,7},{7,3},{8,12},{12,8},{9,1... | collective-permute-start | bytes 786440 | tf_op jit(solution)/shard_map/ppermute | solution.py:90
  13.1 120.2 %reduce-scatter.13.cloned.1.call-start = ((), (), s32[]{:S(2)}) async-start(), calls=%async_computation.9 | async-start | bytes 2621440 | tf_op jit(solution)/shard_map/reduce_scatter | solution.py:72
  19.4 28.7 %collective-permute-start.1 = (bf16[2,128,1024]{2,1,0:T(8,128)(2,1)}, bf16[2,128,1024]{2,1,0:T(8,128)(2,1)S(1)}, u32[]{:S(2)}, u32[]{:S(2)}) collective-permute-start(bf16[2,128,1024]{2,1,0:T(8,128)(2,1)} %pad_maximum_fusion.11), channel_id=1, source_target_pairs={{0,1},{1,2},{2,3},{3,0},{4,5},{5,6},{6,7},{7,4},{8,9},{9,10},{10,1... | collective-permute-start | bytes 1572872 | tf_op jit(solution)/shard_map/ppermute | solution.py:20
  48.1 11.9 %collective-permute-start.3 = (bf16[2,128,1024]{2,1,0:T(8,128)(2,1)}, bf16[2,128,1024]{2,1,0:T(8,128)(2,1)S(1)}, u32[]{:S(2)}, u32[]{:S(2)}) collective-permute-start(bf16[2,128,1024]{2,1,0:T(8,128)(2,1)} %pad_maximum_fusion.11), channel_id=1, source_target_pairs={{0,3},{1,0},{2,1},{3,2},{4,7},{5,4},{6,5},{7,6},{8,11},{9,8},{10,9... | collective-permute-start | bytes 1572872 | tf_op jit(solution)/shard_map/ppermute | solution.py:22
  48.1 14.2 %collective-permute-start.2 = (bf16[2,128,1024]{2,1,0:T(8,128)(2,1)S(1)}, bf16[2,128,1024]{2,1,0:T(8,128)(2,1)}, u32[]{:S(2)}, u32[]{:S(2)}) collective-permute-start(bf16[2,128,1024]{2,1,0:T(8,128)(2,1)S(1)} %collective-permute-done.1), channel_id=1, source_target_pairs={{0,1},{1,2},{2,3},{3,0},{4,5},{5,6},{6,7},{7,4},{8,9},{9,10},{10,1... | collective-permute-start | bytes 1572872 | tf_op jit(solution)/shard_map/ppermute | solution.py:20
  101.5 114.6 %all-gather.7.cloned.1.call-start = ((), (), s32[]{:S(2)}) async-start(), calls=%async_computation.10 | async-start | bytes 5242880 | tf_op jit(solution)/shard_map/all_gather | solution.py:167
  103.9 158.5 %all-gather.9.cloned.1.call-start = ((), (), s32[]{:S(2)}) async-start(), calls=%async_computation.11 | async-start | bytes 2621440 | tf_op jit(solution)/shard_map/all_gather | solution.py:168
  138.1 13.5 %collective-permute-start.4 = (bf16[2,128,1024]{2,1,0:T(8,128)(2,1)S(1)}, bf16[2,128,1024]{2,1,0:T(8,128)(2,1)S(1)}, u32[]{:S(2)}, u32[]{:S(2)}) collective-permute-start(bf16[2,128,1024]{2,1,0:T(8,128)(2,1)S(1)} %multiply_convert_fusion.7), channel_id=1, source_target_pairs={{0,1},{1,2},{2,3},{3,0},{4,5},{5,6},{6,7},{7,4},{8,9},{9,10},{10,1... | collective-permute-start | bytes 1572872 | tf_op jit(solution)/shard_map/ppermute | solution.py:20
  138.2 159.6 %reduce-scatter.15.cloned.1.call-start = ((), (), s32[]{:S(2)}) async-start(), calls=%async_computation.12 | async-start | bytes 2621440 | tf_op jit(solution)/shard_map/reduce_scatter | solution.py:72
  138.2 13.4 %collective-permute-start.6 = (bf16[2,128,1024]{2,1,0:T(8,128)(2,1)S(1)}, bf16[2,128,1024]{2,1,0:T(8,128)(2,1)S(1)}, u32[]{:S(2)}, u32[]{:S(2)}) collective-permute-start(bf16[2,128,1024]{2,1,0:T(8,128)(2,1)S(1)} %multiply_convert_fusion.7), channel_id=1, source_target_pairs={{0,3},{1,0},{2,1},{3,2},{4,7},{5,4},{6,5},{7,6},{8,11},{9,8},{10,9... | collective-permute-start | bytes 1572872 | tf_op jit(solution)/shard_map/ppermute | solution.py:22
  268.3 116.1 %reduce-scatter.17.cloned.1.call-start = ((), (), s32[]{:S(2)}) async-start(), calls=%async_computation.13 | async-start | bytes 2621440 | tf_op jit(solution)/shard_map/reduce_scatter | solution.py:72
  304.6 13.7 %collective-permute-start.9 = (bf16[2,128,1024]{2,1,0:T(8,128)(2,1)S(1)}, bf16[2,128,1024]{2,1,0:T(8,128)(2,1)S(1)}, u32[]{:S(2)}, u32[]{:S(2)}) collective-permute-start(bf16[2,128,1024]{2,1,0:T(8,128)(2,1)S(1)} %fusion.46), channel_id=1, source_target_pairs={{0,1},{1,2},{2,3},{3,0},{4,5},{5,6},{6,7},{7,4},{8,9},{9,10},{10,1... | collective-permute-start | bytes 1572872 | tf_op jit(solution)/shard_map/ppermute | solution.py:20
  304.7 13.6 %collective-permute-start.11 = (bf16[2,128,1024]{2,1,0:T(8,128)(2,1)S(1)}, bf16[2,128,1024]{2,1,0:T(8,128)(2,1)S(1)}, u32[]{:S(2)}, u32[]{:S(2)}) collective-permute-start(bf16[2,128,1024]{2,1,0:T(8,128)(2,1)S(1)} %fusion.46), channel_id=1, source_target_pairs={{0,3},{1,0},{2,1},{3,2},{4,7},{5,4},{6,5},{7,6},{8,11},{9,8},{10,9... | collective-permute-start | bytes 1572872 | tf_op jit(solution)/shard_map/ppermute | solution.py:22
  353.3 123.0 %reduce-scatter.23.cloned.1.call-start = ((), (), s32[]{:S(2)}) async-start(), calls=%async_computation.16 | async-start | bytes 4718592 | tf_op jit(solution)/shard_map/reduce_scatter | solution.py:231
  363.2 184.7 %reduce-scatter.27.cloned.1.call-start = ((), (), s32[]{:S(2)}) async-start(), calls=%async_computation.19 | async-start | bytes 2359296
  390.2 13.5 %collective-permute-start.12 = (bf16[2,128,1024]{2,1,0:T(8,128)(2,1)S(1)}, bf16[2,128,1024]{2,1,0:T(8,128)(2,1)S(1)}, u32[]{:S(2)}, u32[]{:S(2)}) collective-permute-start(bf16[2,128,1024]{2,1,0:T(8,128)(2,1)S(1)} %fusion.47), channel_id=1, source_target_pairs={{0,1},{1,2},{2,3},{3,0},{4,5},{5,6},{6,7},{7,4},{8,9},{9,10},{10,1... | collective-permute-start | bytes 1572872 | tf_op jit(solution)/shard_map/ppermute | solution.py:20
  390.3 21.7 %collective-permute-start.14 = (bf16[2,128,1024]{2,1,0:T(8,128)(2,1)S(1)}, bf16[2,128,1024]{2,1,0:T(8,128)(2,1)}, u32[]{:S(2)}, u32[]{:S(2)}) collective-permute-start(bf16[2,128,1024]{2,1,0:T(8,128)(2,1)S(1)} %fusion.47), channel_id=1, source_target_pairs={{0,3},{1,0},{2,1},{3,2},{4,7},{5,4},{6,5},{7,6},{8,11},{9,8},{10,9... | collective-permute-start | bytes 1572872 | tf_op jit(solution)/shard_map/ppermute | solution.py:22
  403.7 8.7 %collective-permute-start.13 = (bf16[2,128,1024]{2,1,0:T(8,128)(2,1)S(1)}, bf16[2,128,1024]{2,1,0:T(8,128)(2,1)}, u32[]{:S(2)}, u32[]{:S(2)}) collective-permute-start(bf16[2,128,1024]{2,1,0:T(8,128)(2,1)S(1)} %collective-permute-done.12), channel_id=1, source_target_pairs={{0,1},{1,2},{2,3},{3,0},{4,5},{5,6},{6,7},{7,4},{8,9},{9,10},{10,1... | collective-permute-start | bytes 1572872 | tf_op jit(solution)/shard_map/ppermute | solution.py:20
  411.5 201.3 %reduce-scatter.25.cloned.1.call-start = ((), (), s32[]{:S(2)}) async-start(), calls=%async_computation.18 | async-start | bytes 589824
  452.4 228.3 %reduce-scatter.21.cloned.1.call-start = ((), (), s32[]{:S(2)}) async-start(), calls=%async_computation.15 | async-start | bytes 1769472 | tf_op jit(solution)/shard_map/reduce_scatter | solution.py:231
  467.3 245.9 %reduce-scatter.19.cloned.1.call-start = ((), (), s32[]{:S(2)}) async-start(), calls=%async_computation.14 | async-start | bytes 2621440 | tf_op jit(solution)/shard_map/reduce_scatter | solution.py:72
  472.1 263.9 %all-gather.11.cloned.1.call-start = ((), (), s32[]{:S(2)}) async-start(), calls=%async_computation.17 | async-start | bytes 1572864 | tf_op jit(solution)/shard_map/all_gather | solution.py:234
  714.5 24.2 %collective-permute-start.15 = (bf16[128,1024]{1,0:T(8,128)(2,1)S(1)}, bf16[128,1024]{1,0:T(8,128)(2,1)S(1)}, u32[]{:S(2)}, u32[]{:S(2)}) collective-permute-start(bf16[128,1024]{1,0:T(8,128)(2,1)S(1)} %dynamic-slice_bitcast_fusion), channel_id=1, source_target_pairs={{0,4},{4,0},{1,5},{5,1},{2,6},{6,2},{3,7},{7,3},{8,12},{12,8},{9,1... | collective-permute-start | bytes 786440 | tf_op jit(solution)/shard_map/ppermute | solution.py:90
  (69 other events, 1686.9 us)
Sparse Core Ops, SparseCore 0:
  13.2 45.7 all-gather.4
  101.6 31.5 reduce-scatter.12
  135.4 80.7 all-gather.6
  217.6 44.7 all-gather.8
  268.4 29.3 reduce-scatter.14
  353.4 30.9 reduce-scatter.16
  388.0 88.2 reduce-scatter.22
  479.9 67.9 reduce-scatter.26
  551.2 61.6 reduce-scatter.24
  616.1 64.5 reduce-scatter.20
  683.2 29.9 reduce-scatter.18
  714.6 21.2 all-gather.10
